TPU v7x, 32 devices: a whole 2x2x4 slice. The times are simulated.
32 devices in a mesh: grp: 2 (over x), row: 16 (over z, y, core).
Axes of the slice: x: 2, y: 2, z: 4, core: 2. Of those that a mesh axis runs over, the one named last changes fastest.
Arguments:
- alignment: bfloat16 [128, 128, 256], P(('grp', 'row')), parts along dimension 0, may hold values from -6 to 6
- seq_flags: int32 [128], P(('grp', 'row')), parts along dimension 0, may hold values 0 or 1
- crop_flags: int32 [256], P('grp'), parts along dimension 0, may hold values 0 or 1
- norm_gain: float32 [256], replicated, may hold values from 0.5 to 1.5
- norm_bias: float32 [256], replicated, may hold values from -3 to 3
- left_weight: bfloat16 [256, 32], replicated, may hold values from -0.375 to 0.375
- left_bias: float32 [32], replicated, may hold values from -3 to 3
- right_weight: bfloat16 [256, 32], replicated, may hold values from -0.375 to 0.375
- right_bias: float32 [32], replicated, may hold values from -3 to 3
- out_weight: bfloat16 [1024, 128], replicated, may hold values from -0.1875 to 0.1875
- out_bias: float32 [128], replicated, may hold values from -3 to 3
Outputs:
- pair_update: bfloat16 [256, 128, 128], P(('grp', 'row')), parts along dimension 0
There are 2 independent parts, one for each index of `grp`. A program takes and returns all parts, laid end to end along the dimension named above; an argument that names none is the same for every part. Nothing has to cross between parts.
All inputs are finite; a program needn't handle non-finite values. No bound on the sum of `seq_flags` on one device may be relied on, other than what follows from the above.
Results may differ from a plain program's by a relative error of at most 0.004.
Values may be sent and summed in bfloat16 or wider, within the bound.
No kernel may reach another device: no remote copies, remote signals or barrier semaphores. Data moves between devices by JAX's collectives and lax.ppermute only.
A program may use at most 128 MiB of HBM per device.

v0:
```python
import jax
import jax.numpy as jnp
from jax import lax
from jax.sharding import PartitionSpec as P


def normalize(values, norm_gain, norm_bias):
    values = values.astype(jnp.float32)
    average = jnp.mean(values, axis=-1, keepdims=True)
    variance = jnp.mean((values - average) ** 2, axis=-1, keepdims=True)
    return (values - average) * lax.rsqrt(variance + 1e-05) * norm_gain + norm_bias


def project(normed, weight, bias, scaling):
    product = jnp.einsum(
        "src,cd->srd", normed, weight.astype(jnp.float32), precision=lax.Precision.HIGHEST
    )
    return ((product + bias) * scaling).astype(jnp.bfloat16)


def pair_tile(
    left_flat, column_piece, crop_rows, crop_cols, live_count, out_weight, out_bias, channels
):
    rows_here = crop_rows.shape[0]
    width_cols = column_piece.shape[1] // channels
    sums = lax.dot_general(
        left_flat, column_piece, (((0,), (0,)), ((), ())), preferred_element_type=jnp.float32
    )
    outer_sum = sums.reshape(rows_here, channels, width_cols, channels).transpose(0, 2, 1, 3)
    outer_sum = outer_sum.reshape(rows_here * width_cols, channels * channels).astype(jnp.bfloat16)
    projected = jnp.dot(outer_sum, out_weight, preferred_element_type=jnp.float32)
    projected = projected.reshape(rows_here, width_cols, out_weight.shape[1])
    divisor = jnp.maximum(live_count * crop_rows[:, None] * crop_cols[None, :], 1.0)
    return (projected / divisor[:, :, None] + out_bias).astype(jnp.bfloat16)


def column_blocks(
    left_flat, column_piece, crop_rows, crop_cols, live_count, out_weight, out_bias, channels
):
    rows_here = crop_rows.shape[0]
    width_cols = column_piece.shape[1] // channels
    span = max(1, 2048 // rows_here)
    if width_cols > span and width_cols % span == 0:

        def one_block(block_index):
            start = block_index * span
            piece_block = lax.dynamic_slice_in_dim(
                column_piece, start * channels, span * channels, 1
            )
            crop_block = lax.dynamic_slice_in_dim(crop_cols, start, span, 0)
            return pair_tile(
                left_flat,
                piece_block,
                crop_rows,
                crop_block,
                live_count,
                out_weight,
                out_bias,
                channels,
            )

        stacked = lax.map(one_block, jnp.arange(width_cols // span, dtype=jnp.int32))
        return stacked.transpose(1, 0, 2, 3).reshape(rows_here, width_cols, out_weight.shape[1])
    return pair_tile(
        left_flat, column_piece, crop_rows, crop_cols, live_count, out_weight, out_bias, channels
    )


def per_device(
    alignment,
    seq_flags,
    crop_flags,
    norm_gain,
    norm_bias,
    left_weight,
    left_bias,
    right_weight,
    right_bias,
    out_weight,
    out_bias,
):
    channels = left_weight.shape[1]
    devices_row = lax.axis_size("row")
    residues = alignment.shape[1]
    rows_here = residues // devices_row
    crop_float = crop_flags.astype(jnp.float32)
    my_index = lax.axis_index("row")
    crop_rows = lax.dynamic_slice_in_dim(crop_float, my_index * rows_here, rows_here, 0)
    regrouped = lax.all_to_all(alignment, "row", split_axis=1, concat_axis=0, tiled=True)
    all_flags = lax.all_gather(seq_flags, "row", axis=0, tiled=True)
    flag_float = all_flags.astype(jnp.float32)
    live_count = jnp.sum(flag_float)
    normed = normalize(regrouped, norm_gain, norm_bias)
    scaling = flag_float[:, None, None] * crop_rows[None, :, None]
    left = project(normed, left_weight, left_bias, scaling)
    right = project(normed, right_weight, right_bias, scaling)
    sequences = left.shape[0]
    left_flat = left.reshape(sequences, rows_here * channels)
    right_flat = right.reshape(sequences, rows_here * channels)
    return column_blocks(
        left_flat,
        lax.all_gather(right_flat, "row", axis=1, tiled=True),
        crop_rows,
        crop_float,
        live_count,
        out_weight,
        out_bias,
        channels,
    )


def solution(mesh):
    return jax.shard_map(
        per_device,
        mesh=mesh,
        in_specs=(
            P(("grp", "row"), None, None),
            P(("grp", "row")),
            P("grp"),
            P(),
            P(),
            P(),
            P(),
            P(),
            P(),
            P(),
            P(),
        ),
        out_specs=P(("grp", "row"), None, None),
        check_vma=False,
    )
```

profile of v0, /device:TPU:0, one launch (start us, length us, event | category | flops | bytes accessed | tf_op | source)
XLA Modules:
  0.0 54.4 jit_solution(9916558976857848131)
XLA Ops:
  0.0 0.0 copy-start
  0.0 0.0 copy-start.4
  0.0 0.0 copy-start.3
  0.0 1.9 %copy.75 = bf16[4,128,256]{2,0,1:T(4,128)(2,1)} copy(bf16[4,128,256]{2,1,0:T(8,128)(2,1)} %param.11) | data formatting | bytes 524288 | tf_op args[0]
  1.9 7.4 %all-to-all-start = ((bf16[4,128,256]{2,0,1:T(4,128)(2,1)}), bf16[4,128,256]{2,0,1:T(4,128)(2,1)S(1)}, u32[]{:S(2)}, u32[]{:S(2)}) async-start(bf16[4,128,256]{2,0,1:T(4,128)(2,1)} %copy.75), calls=%async_computation | async-start | bytes 524288 | tf_op jit(solution)/shard_map/all_to_all | solution.py:89
  9.3 0.0 copy-start.1
  9.3 0.0 copy-start.5
  9.4 1.3 %dynamic-slice = u32[1]{0:T(128)} dynamic-slice(u32[32]{0:T(128)} %constant.24, u32[]{:T(128)S(6)} %add.58), dynamic_slice_sizes={1} | dynamic-slice | bytes 12
  11.4 0.9 %dynamic-update-slice = s32[64]{0:T(128)S(1)} dynamic-update-slice(s32[64]{0:T(128)S(1)} %broadcast.80, s32[4]{0:T(128)} %param.12, u32[]{:T(128)} %bitcast.7) | dynamic-update-slice | bytes 36
  12.2 12.4 %all-reduce = s32[64]{0:T(128)S(1)} all-reduce(s32[64]{0:T(128)S(1)} %dynamic-update-slice), channel_id=1, replica_groups=mesh['grp'=2,'row'=16] {'row'}, use_global_device_ids=true, to_apply=%add | all-reduce | flops 64 | bytes 512
  24.7 0.7 %convert_reduce_fusion = f32[]{:T(128)} fusion(s32[64]{0:T(128)S(1)} %all-reduce), kind=kLoop, calls=%fused_computation.27 | loop fusion | flops 127 | bytes 260 | tf_op jit(solution)/shard_map/reduce_sum | solution.py:92
  25.4 0.7 %convert_element_type.51 = f32[128]{0:T(128)S(1)} convert(s32[128]{0:T(128)} %param.13) | non-fusion elementwise | flops 128 | bytes 1024 | tf_op jit(solution)/shard_map/convert_element_type | solution.py:86
  26.0 0.8 %broadcast_multiply_fusion.2 = (f32[8]{0:T(128)S(1)}, f32[8]{0:T(128)S(1)}) fusion(f32[]{:T(128)} %convert_reduce_fusion, f32[128]{0:T(128)S(1)} %convert_element_type.51, s32[]{:T(128)S(6)} %select_n.3), kind=kLoop, calls=%fused_computation.26 | loop fusion | flops 8 | bytes 104 | tf_op jit(solution)/shard_map/mul | solution.py:33
  26.8 0.1 multiply_maximum_fusion
  26.9 0.1 broadcast_multiply_fusion
  26.9 0.0 all-to-all-done
  26.9 0.1 fusion.10
  27.1 0.1 copy.79
  27.2 0.1 copy.81
  27.2 0.1 copy.80
  27.3 0.3 multiply_reduce_fusion
  27.6 0.1 copy.83
  27.7 0.1 copy.84
  27.9 0.0 copy-done.4
  27.9 0.0 copy-done.3
  27.9 0.0 copy-start.2
  27.9 0.0 copy-start.6
  27.9 0.2 fusion.9
  28.1 0.0 copy-done.1
  28.1 0.0 copy-done.5
  28.2 0.4 fusion.5
  28.5 0.1 copy.86
  28.7 21.0 %all_gather.7 = bf16[64,4096]{0,1:T(8,128)(2,1)S(1)} all-gather(bf16[64,256]{0,1:T(8,128)(2,1)S(1)} %bitcast.57), channel_id=1, replica_groups=mesh['grp'=2,'row'=16] {'row'}, dimensions={1}, use_global_device_ids=true | all-gather | bytes 557056 | tf_op jit(solution)/shard_map/all_gather | solution.py:102
  49.7 1.1 %copy.87 = bf16[128,32,64]{0,2,1:T(8,128)(2,1)S(1)} copy(bf16[128,32,64]{2,1,0:T(8,128)(2,1)S(1)} %bitcast.55) | data formatting | bytes 1048576 | tf_op jit(solution)/shard_map/dot_general | solution.py:26
  50.8 0.0 copy-done.2
  50.8 0.0 copy-done.6
  50.8 0.4 fusion.4
  51.2 0.1 copy.85
  51.3 0.7 %convert_bitcast_fusion = bf16[8,128,32,32]{1,2,3,0:T(8,128)(2,1)S(1)} fusion(bf16[128,32,64]{0,2,1:T(8,128)(2,1)S(1)} %copy.87, bf16[64,8,32]{0,2,1:T(8,128)(2,1)S(1)} %copy.85), kind=kOutput, calls=%fused_computation | convolution fusion | flops 135266304 | bytes 2654208 | tf_op jit(solution)/shard_map/dot_general | solution.py:26
  52.0 0.0 copy-start.7
  52.0 0.8 %copy.88 = bf16[8,128,32,32]{1,3,2,0:T(8,128)(2,1)S(1)} copy(bf16[8,128,32,32]{1,2,3,0:T(8,128)(2,1)S(1)} %convert_bitcast_fusion) | data formatting | bytes 4194304 | tf_op jit(solution)/shard_map/convert_element_type | solution.py:30
  52.9 0.0 copy-done
  52.9 0.0 copy-done.7
  52.9 1.5 %fusion.1 = bf16[8,128,128]{2,1,0:T(8,128)(2,1)} fusion(bf16[8,128,1024]{1,2,0:T(8,128)(2,1)S(1)} %bitcast.56, bf16[1024,128]{1,0:T(8,128)(2,1)S(1)} %copy-done, f32[128]{0:T(128)S(1)} %copy-done.7, f32[8,128]{1,0:T(8,128)S(1)} %multiply_maximum_fusion), kind=kOutput, calls=%fused_computation.3 | convolution fusion | flops 268828672 | bytes 2626048 | tf_op jit(solution)/shard_map/dot_general | solution.py:31
  (6 shorter events, 0.1 us)
Async XLA Ops:
  0.0 52.9 %copy-start = (bf16[1024,128]{1,0:T(8,128)(2,1)S(1)}, bf16[1024,128]{1,0:T(8,128)(2,1)}, u32[]{:S(2)}) copy-start(bf16[1024,128]{1,0:T(8,128)(2,1)} %param.20) | copy-start | bytes 786436
  0.0 27.9 %copy-start.4 = (f32[256]{0:T(256)S(1)}, f32[256]{0:T(256)}, u32[]{:S(2)}) copy-start(f32[256]{0:T(256)} %param.14) | copy-start | bytes 3076
  0.0 27.9 %copy-start.3 = (f32[256]{0:T(256)S(1)}, f32[256]{0:T(256)}, u32[]{:S(2)}) copy-start(f32[256]{0:T(256)} %param.15) | copy-start | bytes 3076
  1.9 25.0 %all-to-all-start = ((bf16[4,128,256]{2,0,1:T(4,128)(2,1)}), bf16[4,128,256]{2,0,1:T(4,128)(2,1)S(1)}, u32[]{:S(2)}, u32[]{:S(2)}) async-start(bf16[4,128,256]{2,0,1:T(4,128)(2,1)} %copy.75), calls=%async_computation | async-start | bytes 524288 | tf_op jit(solution)/shard_map/all_to_all | solution.py:89
  9.3 18.8 %copy-start.1 = (bf16[256,32]{0,1:T(8,128)(2,1)S(1)}, bf16[256,32]{0,1:T(8,128)(2,1)}, u32[]{:S(2)}) copy-start(bf16[256,32]{0,1:T(8,128)(2,1)} %param.18) | copy-start | bytes 49156
  9.3 18.8 %copy-start.5 = (f32[32]{0:T(128)S(1)}, f32[32]{0:T(128)}, u32[]{:S(2)}) copy-start(f32[32]{0:T(128)} %param.19) | copy-start | bytes 388
  27.9 22.9 %copy-start.2 = (bf16[256,32]{0,1:T(8,128)(2,1)S(1)}, bf16[256,32]{0,1:T(8,128)(2,1)}, u32[]{:S(2)}) copy-start(bf16[256,32]{0,1:T(8,128)(2,1)} %param.16) | copy-start | bytes 49156
  27.9 22.9 %copy-start.6 = (f32[32]{0:T(128)S(1)}, f32[32]{0:T(128)}, u32[]{:S(2)}) copy-start(f32[32]{0:T(128)} %param.17) | copy-start | bytes 388
  52.0 0.8 %copy-start.7 = (f32[128]{0:T(128)S(1)}, f32[128]{0:T(128)}, u32[]{:S(2)}) copy-start(f32[128]{0:T(128)} %param.21) | copy-start | bytes 1540
where the time goes:
time: 54.7 us; the launch traced here: 54.4 us
  blocking collectives  33.5 us (61%)
  starting transfers between devices  7.42 us (14%)
  local copies, waits for them, and re-layouts  6.75 us (12%)
  other arithmetic  2.94 us (5%)
  matrix products  2.91 us (5%)
  between operations  0.9 us (2%)
    all_gather x1, blocking collectives, per_device(): lax.all_gather(right_flat, 'row', axis=1, tiled=True)  21 us
    unnamed x1, blocking collectives  12.4 us
    all_to_all x1, starting transfers between devices, per_device(): lax.all_to_all(alignment, 'row', split_axis=1, concat_axis=0, tiled=True)  7.42 us
    unnamed x20, local copies, waits for them, and re-layouts  4.12 us
    dot_general x1, matrix products, pair_tile(): jnp.dot(outer_sum, out_weight, preferred_element_type=jnp.float32)  1.49 us
    dot_general x1, local copies, waits for them, and re-layouts, pair_tile(): lax.dot_general(left_flat, column_piece, (((0,), (0,)), ((), ())), prefer...  1.11 us
  transfers between devices with their start and end apart: 1, of which 0 were waited for; matrix products, arithmetic and copies ran while one was open for 8% of the time, Pallas kernels for 0%

commit v1 on v0

--- a/solution.py
+++ b/solution.py
@@ -2,6 +2,18 @@
 import jax.numpy as jnp
 from jax import lax
 from jax.sharding import PartitionSpec as P
+
+
+def in_blocks(x, dim, length):
+    shape = x.shape
+    pieces = x.reshape(*shape[:dim], length, shape[dim] // length, *shape[dim + 1 :])
+    return jnp.moveaxis(pieces, dim, 0)
+
+
+def in_order(parts, dim):
+    parts = jnp.moveaxis(parts, 0, dim)
+    shape = parts.shape
+    return parts.reshape(*shape[:dim], shape[dim] * shape[dim + 1], *shape[dim + 2 :])
 
 
 def normalize(values, norm_gain, norm_bias):
@@ -86,7 +98,14 @@
     crop_float = crop_flags.astype(jnp.float32)
     my_index = lax.axis_index("row")
     crop_rows = lax.dynamic_slice_in_dim(crop_float, my_index * rows_here, rows_here, 0)
-    regrouped = lax.all_to_all(alignment, "row", split_axis=1, concat_axis=0, tiled=True)
+    count, position = (lax.axis_size("row"), lax.axis_index("row"))
+    blocks = in_blocks(alignment, 1, count)
+    outs = [blocks[position]]
+    for step in range(1, count):
+        sent = blocks[(position + step) % count]
+        outs.append(lax.ppermute(sent, "row", [(i, (i + step) % count) for i in range(count)]))
+    blocks = jnp.stack(outs)[(position - jnp.arange(count)) % count]
+    regrouped = in_order(blocks, 0)
     all_flags = lax.all_gather(seq_flags, "row", axis=0, tiled=True)
     flag_float = all_flags.astype(jnp.float32)
     live_count = jnp.sum(flag_float)

time: 54.7 us -> 73.1 us (1.34)
  starting transfers between devices: 7.42 us -> 21.2 us
  blocking collectives: 33.5 us -> 36.8 us
  waiting for transfers between devices: 0.01 us -> 1.42 us
    ppermute x0 -> x15, starting transfers between devices: none -> 21.2 us  [per_device(): lax.ppermute(sent, 'row', [(i, (i + step) % count) for i in range(count)])]
    all_to_all x1 -> x0, starting transfers between devices: 7.42 us -> none  [per_device(): lax.all_to_all(alignment, 'row', split_axis=1, concat_axis=0, tiled=True)]
    all_gather x1, blocking collectives: 21 us -> 24.8 us  [per_device(): lax.all_gather(right_flat, 'row', axis=1, tiled=True)]
    ppermute x0 -> x15, waiting for transfers between devices: none -> 1.42 us  [per_device(): lax.ppermute(sent, 'row', [(i, (i + step) % count) for i in range(count)])]
    unnamed x20 -> x34, local copies, waits for them, and re-layouts: 4.12 us -> 2.89 us
    squeeze x0 -> x1, local copies, waits for them, and re-layouts: none -> 0.97 us  [per_device(): sent = blocks[(position + step) % count]]
  transfers between devices with their start and end apart: 1 -> 15, of which waited for: 0 -> 2; matrix products, arithmetic and copies ran while one was open for 8% -> 7% of each run, Pallas kernels for 0% -> 0%
where the time goes in v1:
time: 73.1 us; the launch traced here: 72.9 us
  blocking collectives  36.8 us (50%)
  starting transfers between devices  21.2 us (29%)
  local copies, waits for them, and re-layouts  6.63 us (9%)
  matrix products  2.91 us (4%)
  other arithmetic  2.83 us (4%)
  waiting for transfers between devices  1.42 us (2%)
  between operations  1.13 us (2%)
    all_gather x1, blocking collectives, per_device(): lax.all_gather(right_flat, 'row', axis=1, tiled=True)  24.8 us
    ppermute x15, starting transfers between devices, per_device(): lax.ppermute(sent, 'row', [(i, (i + step) % count) for i in range(count)])  21.2 us
    unnamed x1, blocking collectives  12 us
    unnamed x34, local copies, waits for them, and re-layouts  2.89 us
    dot_general x1, matrix products, pair_tile(): jnp.dot(outer_sum, out_weight, preferred_element_type=jnp.float32)  1.49 us
  transfers between devices with their start and end apart: 15, of which 2 were waited for; matrix products, arithmetic and copies ran while one was open for 7% of the time, Pallas kernels for 0%

profile of v1, /device:TPU:0, one launch (start us, length us, event | category | flops | bytes accessed | tf_op | source)
XLA Modules:
  0.0 72.9 jit_solution(7267451593020646863)
XLA Ops:
  0.2 1.0 %dynamic-slice_bitcast_fusion = (bf16[4,8,256]{2,1,0:T(8,128)(2,1)S(1)}, bf16[4,8,256]{2,1,0:T(8,128)(2,1)S(1)}, bf16[4,8,256]{2,1,0:T(8,128)(2,1)S(1)}, bf16[4,...) fusion(bf16[4,16,8,256]{3,2,1,0:T(8,128)(2,1)} %bitcast.113, ...), kind=kLoop, calls=%fused_computation.41 | loop fusion | bytes 491580 | tf_op jit(solution)/shard_map/squeeze | solution.py:105
  1.2 0.6 collective-permute-start
  1.8 2.6 %collective-permute-start.1 = (bf16[4,8,256]{2,1,0:T(8,128)(2,1)S(1)}, bf16[4,8,256]{2,1,0:T(8,128)(2,1)S(1)}, u32[]{:S(2)}, u32[]{:S(2)}) collective-permute-start(bf16[4,8,256]{2,1,0:T(8,128)(2,1)S(1)} %get-tuple-element.20), channel_id=1, source_target_pairs={{0,2},{1,3},{2,4},{3,5},{4,6},{5,7},{6,8},{7,9},{8,10},{9,11},{10,... | collective-permute-start | bytes 49160 | tf_op jit(solution)/shard_map/ppermute | solution.py:106
  4.3 2.4 %collective-permute-start.2 = (bf16[4,8,256]{2,1,0:T(8,128)(2,1)S(1)}, bf16[4,8,256]{2,1,0:T(8,128)(2,1)S(1)}, u32[]{:S(2)}, u32[]{:S(2)}) collective-permute-start(bf16[4,8,256]{2,1,0:T(8,128)(2,1)S(1)} %get-tuple-element.19), channel_id=1, source_target_pairs={{0,3},{1,4},{2,5},{3,6},{4,7},{5,8},{6,9},{7,10},{8,11},{9,12},{10... | collective-permute-start | bytes 49160 | tf_op jit(solution)/shard_map/ppermute | solution.py:106
  6.7 1.6 %collective-permute-start.3 = (bf16[4,8,256]{2,1,0:T(8,128)(2,1)S(1)}, bf16[4,8,256]{2,1,0:T(8,128)(2,1)S(1)}, u32[]{:S(2)}, u32[]{:S(2)}) collective-permute-start(bf16[4,8,256]{2,1,0:T(8,128)(2,1)S(1)} %get-tuple-element.18), channel_id=1, source_target_pairs={{0,4},{1,5},{2,6},{3,7},{4,8},{5,9},{6,10},{7,11},{8,12},{9,13},{1... | collective-permute-start | bytes 49160 | tf_op jit(solution)/shard_map/ppermute | solution.py:106
  8.3 0.2 collective-permute-start.4
  8.5 1.2 %dynamic-slice.64 = u32[1]{0:T(128)} dynamic-slice(u32[32]{0:T(128)} %constant.129, u32[]{:T(128)S(6)} %add.268), dynamic_slice_sizes={1} | dynamic-slice | bytes 12
  10.4 0.9 %dynamic-update-slice = s32[64]{0:T(128)S(1)} dynamic-update-slice(s32[64]{0:T(128)S(1)} %broadcast.159, s32[4]{0:T(128)} %param.12, u32[]{:T(128)} %bitcast.37) | dynamic-update-slice | bytes 36
  11.3 12.0 %all-reduce = s32[64]{0:T(128)S(1)} all-reduce(s32[64]{0:T(128)S(1)} %dynamic-update-slice), channel_id=1, replica_groups=mesh['grp'=2,'row'=16] {'row'}, use_global_device_ids=true, to_apply=%add | all-reduce | flops 64 | bytes 512
  23.3 0.6 convert_reduce_fusion.1
  23.9 0.7 constant_dynamic-update-slice_fusion.15
  24.6 0.7 convert_element_type.41
  25.3 0.7 broadcast_multiply_fusion.2
  26.0 0.1 multiply_maximum_fusion
  26.1 0.1 broadcast_multiply_fusion
  26.2 0.0 collective-permute-done
  26.2 1.4 %collective-permute-start.5 = (bf16[4,8,256]{2,1,0:T(8,128)(2,1)S(1)}, bf16[4,8,256]{2,1,0:T(8,128)(2,1)S(1)}, u32[]{:S(2)}, u32[]{:S(2)}) collective-permute-start(bf16[4,8,256]{2,1,0:T(8,128)(2,1)S(1)} %get-tuple-element.16), channel_id=1, source_target_pairs={{0,6},{1,7},{2,8},{3,9},{4,10},{5,11},{6,12},{7,13},{8,14},{9,15},... | collective-permute-start | bytes 49160 | tf_op jit(solution)/shard_map/ppermute | solution.py:106
  27.5 0.0 collective-permute-done.2
  27.5 0.5 collective-permute-start.7
  28.1 0.0 collective-permute-done.3
  28.1 2.3 %collective-permute-start.8 = (bf16[4,8,256]{2,1,0:T(8,128)(2,1)S(1)}, bf16[4,8,256]{2,1,0:T(8,128)(2,1)S(1)}, u32[]{:S(2)}, u32[]{:S(2)}) collective-permute-start(bf16[4,8,256]{2,1,0:T(8,128)(2,1)S(1)} %get-tuple-element.13), channel_id=1, source_target_pairs={{0,9},{1,10},{2,11},{3,12},{4,13},{5,14},{6,15},{7,0},{8,1},{9,2},... | collective-permute-start | bytes 49160 | tf_op jit(solution)/shard_map/ppermute | solution.py:106
  30.4 3.3 %collective-permute-start.9 = (bf16[4,8,256]{2,1,0:T(8,128)(2,1)S(1)}, bf16[4,8,256]{2,1,0:T(8,128)(2,1)S(1)}, u32[]{:S(2)}, u32[]{:S(2)}) collective-permute-start(bf16[4,8,256]{2,1,0:T(8,128)(2,1)S(1)} %get-tuple-element.12), channel_id=1, source_target_pairs={{0,10},{1,11},{2,12},{3,13},{4,14},{5,15},{6,0},{7,1},{8,2},{9,3},... | collective-permute-start | bytes 49160 | tf_op jit(solution)/shard_map/ppermute | solution.py:106
  33.7 0.0 collective-permute-done.5
  33.7 0.6 collective-permute-start.10
  34.3 0.0 collective-permute-done.6
  34.3 1.8 %collective-permute-start.11 = (bf16[4,8,256]{2,1,0:T(8,128)(2,1)S(1)}, bf16[4,8,256]{2,1,0:T(8,128)(2,1)S(1)}, u32[]{:S(2)}, u32[]{:S(2)}) collective-permute-start(bf16[4,8,256]{2,1,0:T(8,128)(2,1)S(1)} %get-tuple-element.10), channel_id=1, source_target_pairs={{0,12},{1,13},{2,14},{3,15},{4,0},{5,1},{6,2},{7,3},{8,4},{9,5},{1... | collective-permute-start | bytes 49160 | tf_op jit(solution)/shard_map/ppermute | solution.py:106
  36.1 0.0 collective-permute-done.7
  36.1 0.5 collective-permute-start.12
  36.6 2.3 %collective-permute-start.13 = (bf16[4,8,256]{2,1,0:T(8,128)(2,1)S(1)}, bf16[4,8,256]{2,1,0:T(8,128)(2,1)S(1)}, u32[]{:S(2)}, u32[]{:S(2)}) collective-permute-start(bf16[4,8,256]{2,1,0:T(8,128)(2,1)S(1)} %get-tuple-element.8), channel_id=1, source_target_pairs={{0,14},{1,15},{2,0},{3,1},{4,2},{5,3},{6,4},{7,5},{8,6},{9,7},{10,... | collective-permute-start | bytes 49160 | tf_op jit(solution)/shard_map/ppermute | solution.py:106
  39.0 1.2 %collective-permute-start.14 = (bf16[4,8,256]{2,1,0:T(8,128)(2,1)S(1)}, bf16[4,8,256]{2,1,0:T(8,128)(2,1)S(1)}, u32[]{:S(2)}, u32[]{:S(2)}) collective-permute-start(bf16[4,8,256]{2,1,0:T(8,128)(2,1)S(1)} %get-tuple-element.7), channel_id=1, source_target_pairs={{0,15},{1,0},{2,1},{3,2},{4,3},{5,4},{6,5},{7,6},{8,7},{9,8},{10,9... | collective-permute-start | bytes 49160 | tf_op jit(solution)/shard_map/ppermute | solution.py:106
  40.2 0.2 collective-permute-done.13
  40.4 1.2 %collective-permute-done.14 = bf16[4,8,256]{2,1,0:T(8,128)(2,1)S(1)} collective-permute-done((bf16[4,8,256]{2,1,0:T(8,128)(2,1)S(1)}, bf16[4,8,256]{2,1,0:T(8,128)(2,1)S(1)}, u32[]{:S(2)}, u32[]{:S(2)}) %collective-permute-start.14) | collective-permute-done | bytes 16416 | tf_op jit(solution)/shard_map/ppermute | solution.py:106
  41.6 0.6 gather_fusion
  42.2 0.2 convert_reduce_fusion
  42.4 0.3 multiply_reduce_fusion
  42.7 0.0 copy-start.2
  42.7 0.0 copy-start.6
  42.7 0.2 fusion.9
  42.9 0.4 fusion.5
  43.3 0.1 copy.14
  43.5 24.8 %all_gather.7 = bf16[64,4096]{0,1:T(8,128)(2,1)S(1)} all-gather(bf16[64,256]{0,1:T(8,128)(2,1)S(1)} %bitcast.112), channel_id=1, replica_groups=mesh['grp'=2,'row'=16] {'row'}, dimensions={1}, use_global_device_ids=true | all-gather | bytes 557056 | tf_op jit(solution)/shard_map/all_gather | solution.py:121
  68.2 1.1 %copy.15 = bf16[128,32,64]{0,2,1:T(8,128)(2,1)S(1)} copy(bf16[128,32,64]{2,1,0:T(8,128)(2,1)S(1)} %bitcast.109) | data formatting | bytes 1048576 | tf_op jit(solution)/shard_map/dot_general | solution.py:38
  69.3 0.4 fusion.4
  69.7 0.1 copy.13
  69.8 0.7 convert_bitcast_fusion
  70.5 0.0 copy-start.7
  70.5 0.8 %copy.16 = bf16[8,128,32,32]{1,3,2,0:T(8,128)(2,1)S(1)} copy(bf16[8,128,32,32]{1,2,3,0:T(8,128)(2,1)S(1)} %convert_bitcast_fusion) | data formatting | bytes 4194304 | tf_op jit(solution)/shard_map/convert_element_type | solution.py:42
  71.4 1.5 %fusion.1 = bf16[8,128,128]{2,1,0:T(8,128)(2,1)} fusion(bf16[8,128,1024]{1,2,0:T(8,128)(2,1)S(1)} %bitcast.110, bf16[1024,128]{1,0:T(8,128)(2,1)S(1)} %copy-done, f32[128]{0:T(128)S(1)} %copy-done.7, f32[8,128]{1,0:T(8,128)S(1)} %multiply_maximum_fusion), kind=kOutput, calls=%fused_computation.4 | convolution fusion | flops 268828672 | bytes 2626048 | tf_op jit(solution)/shard_map/dot_general | solution.py:43
  (42 shorter events, 0.1 us)
Async XLA Ops:
  0.0 71.4 %copy-start = (bf16[1024,128]{1,0:T(8,128)(2,1)S(1)}, bf16[1024,128]{1,0:T(8,128)(2,1)}, u32[]{:S(2)}) copy-start(bf16[1024,128]{1,0:T(8,128)(2,1)} %param.20) | copy-start | bytes 786436
  0.0 42.7 %copy-start.4 = (f32[256]{0:T(256)S(1)}, f32[256]{0:T(256)}, u32[]{:S(2)}) copy-start(f32[256]{0:T(256)} %param.14) | copy-start | bytes 3076
  0.0 42.7 %copy-start.3 = (f32[256]{0:T(256)S(1)}, f32[256]{0:T(256)}, u32[]{:S(2)}) copy-start(f32[256]{0:T(256)} %param.15) | copy-start | bytes 3076
  0.0 42.9 %copy-start.1 = (bf16[256,32]{0,1:T(8,128)(2,1)S(1)}, bf16[256,32]{0,1:T(8,128)(2,1)}, u32[]{:S(2)}) copy-start(bf16[256,32]{0,1:T(8,128)(2,1)} %param.18) | copy-start | bytes 49156
  0.0 42.9 %copy-start.5 = (f32[32]{0:T(128)S(1)}, f32[32]{0:T(128)}, u32[]{:S(2)}) copy-start(f32[32]{0:T(128)} %param.19) | copy-start | bytes 388
  1.2 25.0 %collective-permute-start = (bf16[4,8,256]{2,1,0:T(8,128)(2,1)S(1)}, bf16[4,8,256]{2,1,0:T(8,128)(2,1)S(1)}, u32[]{:S(2)}, u32[]{:S(2)}) collective-permute-start(bf16[4,8,256]{2,1,0:T(8,128)(2,1)S(1)} %get-tuple-element.21), channel_id=1, source_target_pairs={{0,1},{1,2},{2,3},{3,4},{4,5},{5,6},{6,7},{7,8},{8,9},{9,10},{10,1... | collective-permute-start | bytes 49160 | tf_op jit(solution)/shard_map/ppermute | solution.py:106
  1.8 25.8 %collective-permute-start.1 = (bf16[4,8,256]{2,1,0:T(8,128)(2,1)S(1)}, bf16[4,8,256]{2,1,0:T(8,128)(2,1)S(1)}, u32[]{:S(2)}, u32[]{:S(2)}) collective-permute-start(bf16[4,8,256]{2,1,0:T(8,128)(2,1)S(1)} %get-tuple-element.20), channel_id=1, source_target_pairs={{0,2},{1,3},{2,4},{3,5},{4,6},{5,7},{6,8},{7,9},{8,10},{9,11},{10,... | collective-permute-start | bytes 49160 | tf_op jit(solution)/shard_map/ppermute | solution.py:106
  4.3 23.2 %collective-permute-start.2 = (bf16[4,8,256]{2,1,0:T(8,128)(2,1)S(1)}, bf16[4,8,256]{2,1,0:T(8,128)(2,1)S(1)}, u32[]{:S(2)}, u32[]{:S(2)}) collective-permute-start(bf16[4,8,256]{2,1,0:T(8,128)(2,1)S(1)} %get-tuple-element.19), channel_id=1, source_target_pairs={{0,3},{1,4},{2,5},{3,6},{4,7},{5,8},{6,9},{7,10},{8,11},{9,12},{10... | collective-permute-start | bytes 49160 | tf_op jit(solution)/shard_map/ppermute | solution.py:106
  6.7 21.3 %collective-permute-start.3 = (bf16[4,8,256]{2,1,0:T(8,128)(2,1)S(1)}, bf16[4,8,256]{2,1,0:T(8,128)(2,1)S(1)}, u32[]{:S(2)}, u32[]{:S(2)}) collective-permute-start(bf16[4,8,256]{2,1,0:T(8,128)(2,1)S(1)} %get-tuple-element.18), channel_id=1, source_target_pairs={{0,4},{1,5},{2,6},{3,7},{4,8},{5,9},{6,10},{7,11},{8,12},{9,13},{1... | collective-permute-start | bytes 49160 | tf_op jit(solution)/shard_map/ppermute | solution.py:106
  8.3 22.0 %collective-permute-start.4 = (bf16[4,8,256]{2,1,0:T(8,128)(2,1)S(1)}, bf16[4,8,256]{2,1,0:T(8,128)(2,1)S(1)}, u32[]{:S(2)}, u32[]{:S(2)}) collective-permute-start(bf16[4,8,256]{2,1,0:T(8,128)(2,1)S(1)} %get-tuple-element.17), channel_id=1, source_target_pairs={{0,5},{1,6},{2,7},{3,8},{4,9},{5,10},{6,11},{7,12},{8,13},{9,14},{... | collective-permute-start | bytes 49160 | tf_op jit(solution)/shard_map/ppermute | solution.py:106
  26.2 7.5 %collective-permute-start.5 = (bf16[4,8,256]{2,1,0:T(8,128)(2,1)S(1)}, bf16[4,8,256]{2,1,0:T(8,128)(2,1)S(1)}, u32[]{:S(2)}, u32[]{:S(2)}) collective-permute-start(bf16[4,8,256]{2,1,0:T(8,128)(2,1)S(1)} %get-tuple-element.16), channel_id=1, source_target_pairs={{0,6},{1,7},{2,8},{3,9},{4,10},{5,11},{6,12},{7,13},{8,14},{9,15},... | collective-permute-start | bytes 49160 | tf_op jit(solution)/shard_map/ppermute | solution.py:106
  27.5 6.8 %collective-permute-start.6 = (bf16[4,8,256]{2,1,0:T(8,128)(2,1)S(1)}, bf16[4,8,256]{2,1,0:T(8,128)(2,1)S(1)}, u32[]{:S(2)}, u32[]{:S(2)}) collective-permute-start(bf16[4,8,256]{2,1,0:T(8,128)(2,1)S(1)} %get-tuple-element.15), channel_id=1, source_target_pairs={{0,7},{1,8},{2,9},{3,10},{4,11},{5,12},{6,13},{7,14},{8,15},{9,0},... | collective-permute-start | bytes 49160 | tf_op jit(solution)/shard_map/ppermute | solution.py:106
  27.5 8.6 %collective-permute-start.7 = (bf16[4,8,256]{2,1,0:T(8,128)(2,1)S(1)}, bf16[4,8,256]{2,1,0:T(8,128)(2,1)S(1)}, u32[]{:S(2)}, u32[]{:S(2)}) collective-permute-start(bf16[4,8,256]{2,1,0:T(8,128)(2,1)S(1)} %get-tuple-element.14), channel_id=1, source_target_pairs={{0,8},{1,9},{2,10},{3,11},{4,12},{5,13},{6,14},{7,15},{8,0},{9,1},... | collective-permute-start | bytes 49160 | tf_op jit(solution)/shard_map/ppermute | solution.py:106
  28.1 8.6 %collective-permute-start.8 = (bf16[4,8,256]{2,1,0:T(8,128)(2,1)S(1)}, bf16[4,8,256]{2,1,0:T(8,128)(2,1)S(1)}, u32[]{:S(2)}, u32[]{:S(2)}) collective-permute-start(bf16[4,8,256]{2,1,0:T(8,128)(2,1)S(1)} %get-tuple-element.13), channel_id=1, source_target_pairs={{0,9},{1,10},{2,11},{3,12},{4,13},{5,14},{6,15},{7,0},{8,1},{9,2},... | collective-permute-start | bytes 49160 | tf_op jit(solution)/shard_map/ppermute | solution.py:106
  30.4 8.6 %collective-permute-start.9 = (bf16[4,8,256]{2,1,0:T(8,128)(2,1)S(1)}, bf16[4,8,256]{2,1,0:T(8,128)(2,1)S(1)}, u32[]{:S(2)}, u32[]{:S(2)}) collective-permute-start(bf16[4,8,256]{2,1,0:T(8,128)(2,1)S(1)} %get-tuple-element.12), channel_id=1, source_target_pairs={{0,10},{1,11},{2,12},{3,13},{4,14},{5,15},{6,0},{7,1},{8,2},{9,3},... | collective-permute-start | bytes 49160 | tf_op jit(solution)/shard_map/ppermute | solution.py:106
  33.7 6.5 %collective-permute-start.10 = (bf16[4,8,256]{2,1,0:T(8,128)(2,1)S(1)}, bf16[4,8,256]{2,1,0:T(8,128)(2,1)S(1)}, u32[]{:S(2)}, u32[]{:S(2)}) collective-permute-start(bf16[4,8,256]{2,1,0:T(8,128)(2,1)S(1)} %get-tuple-element.11), channel_id=1, source_target_pairs={{0,11},{1,12},{2,13},{3,14},{4,15},{5,0},{6,1},{7,2},{8,3},{9,4},{... | collective-permute-start | bytes 49160 | tf_op jit(solution)/shard_map/ppermute | solution.py:106
  34.3 5.8 %collective-permute-start.11 = (bf16[4,8,256]{2,1,0:T(8,128)(2,1)S(1)}, bf16[4,8,256]{2,1,0:T(8,128)(2,1)S(1)}, u32[]{:S(2)}, u32[]{:S(2)}) collective-permute-start(bf16[4,8,256]{2,1,0:T(8,128)(2,1)S(1)} %get-tuple-element.10), channel_id=1, source_target_pairs={{0,12},{1,13},{2,14},{3,15},{4,0},{5,1},{6,2},{7,3},{8,4},{9,5},{1... | collective-permute-start | bytes 49160 | tf_op jit(solution)/shard_map/ppermute | solution.py:106
  36.1 4.0 %collective-permute-start.12 = (bf16[4,8,256]{2,1,0:T(8,128)(2,1)S(1)}, bf16[4,8,256]{2,1,0:T(8,128)(2,1)S(1)}, u32[]{:S(2)}, u32[]{:S(2)}) collective-permute-start(bf16[4,8,256]{2,1,0:T(8,128)(2,1)S(1)} %get-tuple-element.9), channel_id=1, source_target_pairs={{0,13},{1,14},{2,15},{3,0},{4,1},{5,2},{6,3},{7,4},{8,5},{9,6},{10... | collective-permute-start | bytes 49160 | tf_op jit(solution)/shard_map/ppermute | solution.py:106
  36.6 3.8 %collective-permute-start.13 = (bf16[4,8,256]{2,1,0:T(8,128)(2,1)S(1)}, bf16[4,8,256]{2,1,0:T(8,128)(2,1)S(1)}, u32[]{:S(2)}, u32[]{:S(2)}) collective-permute-start(bf16[4,8,256]{2,1,0:T(8,128)(2,1)S(1)} %get-tuple-element.8), channel_id=1, source_target_pairs={{0,14},{1,15},{2,0},{3,1},{4,2},{5,3},{6,4},{7,5},{8,6},{9,7},{10,... | collective-permute-start | bytes 49160 | tf_op jit(solution)/shard_map/ppermute | solution.py:106
  39.0 2.6 %collective-permute-start.14 = (bf16[4,8,256]{2,1,0:T(8,128)(2,1)S(1)}, bf16[4,8,256]{2,1,0:T(8,128)(2,1)S(1)}, u32[]{:S(2)}, u32[]{:S(2)}) collective-permute-start(bf16[4,8,256]{2,1,0:T(8,128)(2,1)S(1)} %get-tuple-element.7), channel_id=1, source_target_pairs={{0,15},{1,0},{2,1},{3,2},{4,3},{5,4},{6,5},{7,6},{8,7},{9,8},{10,9... | collective-permute-start | bytes 49160 | tf_op jit(solution)/shard_map/ppermute | solution.py:106
  42.7 26.6 %copy-start.2 = (bf16[256,32]{0,1:T(8,128)(2,1)S(1)}, bf16[256,32]{0,1:T(8,128)(2,1)}, u32[]{:S(2)}) copy-start(bf16[256,32]{0,1:T(8,128)(2,1)} %param.16) | copy-start | bytes 49156
  42.7 26.6 %copy-start.6 = (f32[32]{0:T(128)S(1)}, f32[32]{0:T(128)}, u32[]{:S(2)}) copy-start(f32[32]{0:T(128)} %param.17) | copy-start | bytes 388
  70.5 0.8 %copy-start.7 = (f32[128]{0:T(128)S(1)}, f32[128]{0:T(128)}, u32[]{:S(2)}) copy-start(f32[128]{0:T(128)} %param.21) | copy-start | bytes 1540
